TPU v7x, 32 devices: a whole 2x2x4 slice. The times are simulated.
32 devices in a mesh: dp: 2 (over x), cp: 4 (over z), tensor: 4 (over y, core).
Axes of the slice: x: 2, y: 2, z: 4, core: 2. Of those that a mesh axis runs over, the one named last changes fastest.
Arguments:
- x_in: bfloat16 [8192, 2048], P('tensor', ('dp', 'cp')), parts along dimension 1, may hold values from -6 to 6
- z_gate: bfloat16 [8192, 2048], P('tensor', ('dp', 'cp')), parts along dimension 1, may hold values from -6 to 6
- bc_in: bfloat16 [8, 256, 2048], P(None, None, ('dp', 'cp')), parts along dimension 2, may hold values from -6 to 6
- dt_raw: bfloat16 [128, 2048], P('tensor', ('dp', 'cp')), parts along dimension 1, may hold values from -3 to 13
- conv_x_w: float32 [8192, 4], P('tensor'), may hold values from -3 to 3
- conv_x_b: float32 [8192], P('tensor'), may hold values from -1.7 to 0.3
- conv_bc_w: float32 [8, 256, 4], replicated, may hold values from -3 to 3
- conv_bc_b: float32 [8, 256], replicated, may hold values from -1.7 to 0.3
- dt_bias: float32 [128], P('tensor'), may hold values from -10 to -1.5
- a_log: float32 [128], P('tensor'), may hold values from -4.6 to -2
- d_skip: float32 [128], P('tensor'), may hold values from 0.5 to 2
Outputs:
- y_out: bfloat16 [8192, 2048], P('tensor', ('dp', 'cp')), parts along dimension 1
There are 2 independent parts, one for each index of `dp`. A program takes and returns all parts, laid end to end along the dimension named above; an argument that names none is the same for every part. Nothing has to cross between parts.
All inputs are finite; a program needn't handle non-finite values.
Results may differ from a plain program's by a relative error of at most 0.0085.
Values may be sent and summed in bfloat16 or wider, within the bound.
A program may use at most 64 MiB of HBM per device.

v0:
```python
import math

import jax
import jax.numpy as jnp
from jax import lax
from jax.sharding import PartitionSpec as P

HEADS = 128
GROUPS = 8
BLOCK = 256


def passed_along(block, axis, distance):
    devices = range(lax.axis_size(axis))
    route = [(i - distance, i) for i in devices if i - distance in devices]
    return lax.ppermute(block, axis, route)


def prefix(part, axis, combine, identity):
    place = lax.axis_index(axis)
    gathered = jax.tree.map(lambda a: lax.all_gather(a, axis), part)
    state = jax.tree.map(lambda a, e: jnp.zeros_like(a) + jnp.asarray(e, a.dtype), part, identity)

    def one(step, state):
        return combine(
            state, jax.tree.map(lambda a: lax.dynamic_index_in_dim(a, step, 0, False), gathered)
        )

    return lax.fori_loop(0, place, one, state)


def causal_filter(series, taps, offsets, history):
    kernel_size = taps.shape[-1]
    length = series.shape[-1]
    padded = jnp.concatenate([history, series], axis=-1)
    summed = jnp.broadcast_to(offsets[..., None], series.shape)
    for tap_index in range(kernel_size):
        summed = (
            summed
            + taps[..., tap_index : tap_index + 1] * padded[..., tap_index : tap_index + length]
        )
    return jax.nn.silu(summed)


def block_prep(x_values, step_size, rates, b_rows):
    unit_count, channels, length = x_values.shape
    groups = b_rows.shape[0]
    nblocks = length // BLOCK
    cumulative = jnp.cumsum(
        (step_size * rates[:, None]).reshape(unit_count, nblocks, BLOCK), axis=2
    )
    block_ends = cumulative[:, :, BLOCK - 1]
    input_gain = step_size.reshape(unit_count, nblocks, BLOCK) * jnp.exp(
        block_ends[:, :, None] - cumulative
    )
    weighted = (
        x_values.astype(jnp.float32).reshape(unit_count, channels, nblocks, BLOCK)
        * input_gain[:, None]
    ).astype(jnp.bfloat16)
    weighted = weighted.reshape(groups, unit_count // groups * channels, nblocks, BLOCK)
    b_split = b_rows.reshape(groups, b_rows.shape[1], nblocks, BLOCK)
    states = jnp.einsum("gcbs,gnbs->gbcn", weighted, b_split, preferred_element_type=jnp.float32)
    states = states.reshape(groups, nblocks, unit_count // groups, channels, b_rows.shape[1])
    states = jnp.moveaxis(states, 1, 2).reshape(unit_count, nblocks, channels, b_rows.shape[1])
    return (cumulative, block_ends, states)


def carry_blocks(block_ends, states):

    def advance(carried, inputs):
        decay, new_state = inputs
        return (jnp.exp(decay)[:, None, None] * carried + new_state, carried)

    last_state, entering = lax.scan(
        advance, jnp.zeros_like(states[:, 0]), (block_ends.T, jnp.moveaxis(states, 1, 0))
    )
    return (jnp.moveaxis(entering, 0, 1), last_state)


def state_output(c_rows, entering, cumulative):
    unit_count, nblocks, channels, state_dim = entering.shape
    groups = c_rows.shape[0]
    per_group = unit_count // groups
    rounded = entering.astype(jnp.bfloat16).reshape(groups, per_group, nblocks, channels, state_dim)
    rounded = jnp.moveaxis(rounded, 2, 1).reshape(groups, nblocks, per_group * channels, state_dim)
    c_split = c_rows.reshape(groups, state_dim, nblocks, BLOCK)
    product = jnp.einsum("gbcn,gnbt->gcbt", rounded, c_split, preferred_element_type=jnp.float32)
    product = product.reshape(unit_count, channels, nblocks, BLOCK) * jnp.exp(cumulative)[:, None]
    return product.reshape(unit_count, channels, nblocks * BLOCK)


def intra_output(x_values, step_size, cumulative, b_rows, c_rows):
    unit_count, channels, length = x_values.shape
    groups = b_rows.shape[0]
    state_dim = b_rows.shape[1]
    per_group = unit_count // groups
    nblocks = length // BLOCK
    step_blocks = math.gcd(nblocks, max(1, 1024 // BLOCK))
    rows_step = step_blocks * BLOCK
    causal = lax.broadcasted_iota(jnp.int32, (BLOCK, BLOCK), 0) >= lax.broadcasted_iota(
        jnp.int32, (BLOCK, BLOCK), 1
    )

    def one_step(index, result):
        x_part = x_values.reshape(groups, per_group, channels, step_blocks, BLOCK)
        d_part = step_size.reshape(groups, per_group, step_blocks, BLOCK)
        cum_part = cumulative.reshape(groups, per_group, step_blocks, BLOCK)
        b_part = b_rows.reshape(groups, state_dim, step_blocks, BLOCK)
        c_part = c_rows.reshape(groups, state_dim, step_blocks, BLOCK)
        gram = jnp.einsum("gnbt,gnbs->gbts", c_part, b_part, preferred_element_type=jnp.float32)
        spread = cum_part[..., :, None] - cum_part[..., None, :]
        decayed = jnp.where(causal, jnp.exp(jnp.where(causal, spread, 0.0)), 0.0)
        mixing = (gram[:, None] * decayed * d_part[..., None, :]).astype(jnp.bfloat16)
        y_part = jnp.einsum(
            "gucbs,gubts->gucbt", x_part, mixing, preferred_element_type=jnp.float32
        )
        return y_part.reshape(unit_count, channels, rows_step)

    return lax.fori_loop(
        0, nblocks // step_blocks, one_step, jnp.zeros((unit_count, channels, length), jnp.float32)
    )


def join_states(earlier, later):
    return (earlier[0] * later[0], later[0][:, None, None] * earlier[1] + later[1])


def local(
    x_in, z_gate, bc_in, dt_raw, conv_x_w, conv_x_b, conv_bc_w, conv_bc_b, dt_bias, a_log, d_skip
):
    heads_here = dt_raw.shape[0]
    tok_here = dt_raw.shape[1]
    head_dim = x_in.shape[0] // heads_here
    state_dim = bc_in.shape[1] // 2
    kernel_size = conv_x_w.shape[1]
    group_heads = HEADS // GROUPS
    local_groups = max(1, heads_here // group_heads)
    first_group = lax.axis_index("tensor") * heads_here // group_heads
    bc_mine = lax.dynamic_slice_in_dim(bc_in, first_group, local_groups, 0)
    taps_mine = lax.dynamic_slice_in_dim(conv_bc_w, first_group, local_groups, 0)
    offsets_mine = lax.dynamic_slice_in_dim(conv_bc_b, first_group, local_groups, 0)
    rates = -jnp.exp(a_log)
    rim_values = passed_along(
        (x_in[:, tok_here - kernel_size + 1 :], bc_mine[:, :, tok_here - kernel_size + 1 :]),
        "cp",
        1,
    )
    x_conv = causal_filter(
        x_in.astype(jnp.float32), conv_x_w, conv_x_b, rim_values[0].astype(jnp.float32)
    ).astype(jnp.bfloat16)
    bc_conv = causal_filter(
        bc_mine.astype(jnp.float32), taps_mine, offsets_mine, rim_values[1].astype(jnp.float32)
    ).astype(jnp.bfloat16)
    x_values = x_conv.reshape(heads_here, head_dim, tok_here)
    step_size = jax.nn.softplus(dt_raw.astype(jnp.float32) + dt_bias[:, None])
    b_rows = bc_conv[:, :state_dim]
    c_rows = bc_conv[:, state_dim:]
    cumulative, block_ends, states = block_prep(x_values, step_size, rates, b_rows)
    local_entering, last_state = carry_blocks(block_ends, states)
    total_decay = jnp.exp(jnp.sum(block_ends, axis=1))
    incoming = prefix(
        (total_decay, last_state),
        "cp",
        join_states,
        (jnp.ones_like(total_decay), jnp.zeros_like(last_state)),
    )[1]
    local_part = intra_output(x_values, step_size, cumulative, b_rows, c_rows) + d_skip[
        :, None, None
    ] * x_values.astype(jnp.float32)
    prior_decay = jnp.exp(jnp.cumsum(block_ends, axis=1) - block_ends)
    entering = local_entering + prior_decay[:, :, None, None] * incoming[:, None]
    mixed_out = local_part + state_output(c_rows, entering, cumulative)
    y_tokens = lax.optimization_barrier(
        mixed_out.astype(jnp.bfloat16).reshape(heads_here * head_dim, tok_here)
    )
    return (y_tokens.astype(jnp.float32) * jax.nn.silu(z_gate.astype(jnp.float32))).astype(
        jnp.bfloat16
    )


def solution(mesh):
    return jax.shard_map(
        local,
        mesh=mesh,
        in_specs=(
            P("tensor", ("dp", "cp")),
            P("tensor", ("dp", "cp")),
            P(None, None, ("dp", "cp")),
            P("tensor", ("dp", "cp")),
            P("tensor", None),
            P("tensor"),
            P(),
            P(),
            P("tensor"),
            P("tensor"),
            P("tensor"),
        ),
        out_specs=P("tensor", ("dp", "cp")),
        check_vma=False,
    )
```

profile of v0, /device:TPU:24, one launch (start us, length us, event | category | flops | bytes accessed | tf_op | source)
XLA Modules:
  0.0 131.4 jit_solution(5937542275489967418)
XLA Ops:
  6.5 0.0 copy-start
  6.5 0.0 copy-start.1
  6.5 0.0 copy-start.8
  6.5 0.0 copy-start.3
  6.5 0.0 copy-start.6
  6.5 0.0 copy-start.4
  6.6 0.0 all-gather.3.cloned.1.call-start
  6.6 1.1 constant_dynamic-slice_fusion.2
  7.7 1.3 collective-permute-start
  9.0 1.3 slice.76
  10.3 1.3 collective-permute-start.1
  11.6 1.0 dynamic-slice_convert_fusion
  12.6 0.0 copy-done.8
  12.6 0.0 copy-done.3
  12.6 0.0 copy-done.6
  12.6 0.1 broadcast_multiply_fusion
  12.7 0.6 reduce-window.6
  13.3 0.2 slice_reduce_fusion
  13.6 0.1 copy.34
  13.7 0.0 copy-done.4
  13.7 0.9 constant_dynamic-slice_fusion.3
  14.6 0.1 broadcast.94
  14.7 0.9 multiply_reduce_fusion
  15.6 0.1 fusion.39
  15.7 0.0 copy-done
  15.8 0.0 copy-done.1
  15.8 0.2 convert_element_type.71
  15.9 0.0 copy-start.5
  15.9 0.0 collective-permute-done
  16.0 1.0 multiply_convert_fusion.4
  17.0 9.5 %collective-permute-done.1 = bf16[2048,3]{1,0:T(8,128)(2,1)S(1)} collective-permute-done((bf16[2048,3]{1,0:T(8,128)(2,1)S(1)}, bf16[2048,3]{1,0:T(8,128)(2,1)S(1)}, u32[]{:S(2)}, u32[]{:S(2)}) %collective-permute-start.1) | collective-permute-done | bytes 12320 | tf_op jit(solution)/shard_map/ppermute | solution.py:16
  26.5 0.1 convert_element_type.70
  26.5 0.0 copy-done.5
  26.5 4.0 %multiply_convert_fusion.2 = bf16[2048,256]{1,0:T(8,128)(2,1)S(1)} fusion(f32[2048,256]{1,0:T(8,128)S(1)} %convert_element_type.71, f32[2048,3]{1,0:T(8,128)S(1)} %convert_element_type.70, f32[2048]{0:T(1024)S(1)} %bitcast.89, f32[2048]{0:T(1024)S(1)} %bitcast.90, f32[2048]{0:T(1024)S(1)} %bitcast.88, f32[2048]{0:T(1024)S(1)} %bitcast.87, f32[2048]{0:T(1024)S(1)} %copy-done.5), kind=kLoop, calls=%fused_computation.36 | loop fusion | flops 8388608 | bytes 3211264 | tf_op jit(solution)/shard_map/convert_element_type | solution.py:150
  30.6 0.2 mul.265
  30.7 0.3 fusion.22
  31.1 0.4 fusion.33
  31.5 0.0 copy-start.9
  31.5 0.0 copy-start.7
  31.5 1.1 broadcast_add_fusion
  32.6 0.0 all-gather.3.cloned.1.call-update
  32.7 0.0 copy-done.9
  32.8 0.7 dynamic-slice
  34.1 0.2 dynamic-update-slice
  34.4 8.3 %all-reduce = f32[128]{0:T(128)S(1)} all-reduce(f32[128]{0:T(128)S(1)} %dynamic-update-slice), channel_id=2, replica_groups=mesh['dp'=2,'cp'=4,'tensor'=4] {'cp'}, use_global_device_ids=true, to_apply=%add | all-reduce | flops 128 | bytes 1024
  42.6 0.1 reshape.249
  42.7 0.0 copy-done.7
  42.7 0.1 mul.256
  42.8 0.1 mul.257
  42.9 0.3 fusion.35
  43.2 4.3 %fusion = f32[2,16,256,64]{2,3,1,0:T(8,128)} fusion(bf16[2,16,64,256]{3,2,1,0:T(8,128)(2,1)S(1)} %bitcast.79, f32[2,16,256]{2,1,0:T(8,128)S(1)} %bitcast.91, f32[2,16,256]{2,1,0:T(8,128)S(1)} %reduce_window_sum.45, f32[2,256,256]{2,1,0:T(8,128)S(1)} %fusion.35, pred[256,256]{1,0:T(8,128)(4,1)S(1)} %iota_compare_fusion), kind=kOutput, calls=%fused_computation.3 | convolution fusion | flops 281018368 | bytes 3801088 | tf_op jit(solution)/shard_map/while/body/eval_jaxpr/gucbs,gubts->gucbt/dot_general | solution.py:114
  47.5 64.6 %all-gather.3.cloned.1.call-done = f32[4,32,64,128]{3,2,1,0:T(8,128)} async-done(((f32[1,32,64,128]{3,2,1,0:T(8,128)}), f32[4,32,64,128]{3,2,1,0:T(8,128)}) %all-gather.3.cloned.1.call-update) | async-done | bytes 4194320 | tf_op jit(solution)/shard_map/all_gather | solution.py:21
  112.1 0.1 broadcast.95
  112.2 4.5 %while.3 = (s32[]{:T(128)}, f32[32,64,128]{2,1,0:T(8,128)S(1)}, s32[]{:T(128)}, f32[4,32]{1,0:T(4,128)S(1)}, f32[4,32,64,128]{3,2,1,0:T(8,128)}, /*index=5*/s32[]{:T(128)}, s32[]{:T(128)}, s32[]{:T(128)}) while((s32[]{:T(128)}, f32[32,64,128]{2,1,0:T(8,128)S(1)}, s32[]{:T(128)}, f32[4,32]{1,0:T(4,128)S(1)}, f32[4,32,64,128]{3,2,1,0:T(8,128)}, ...), condition=%wide.region_3.4_spmd, body=%wide.region_2.3_spmd.sunk | while | flops 524293 | bytes 3146239 | solution.py:29
  112.3 1.5 %bitcast_add_fusion.4 = f32[32,64,128]{2,1,0:T(8,128)S(1)} fusion(f32[4,32,64,128]{3,2,1,0:T(8,128)} %get-tuple-element.168, s32[]{:T(128)S(6)} %select_n.51, f32[32,64,128]{2,1,0:T(8,128)S(1)} %get-tuple-element.157, f32[32]{0:T(128)S(1)} %dynamic-slice_bitcast_fusion.2), kind=kLoop, calls=%fused_computation.clone.1 | loop fusion | flops 524288 | bytes 3145860 | tf_op jit(solution)/shard_map/while/body/add | solution.py:125
  113.8 1.5 %bitcast_add_fusion.4 = f32[32,64,128]{2,1,0:T(8,128)S(1)} fusion(f32[4,32,64,128]{3,2,1,0:T(8,128)} %get-tuple-element.168, s32[]{:T(128)S(6)} %select_n.51, f32[32,64,128]{2,1,0:T(8,128)S(1)} %get-tuple-element.157, f32[32]{0:T(128)S(1)} %dynamic-slice_bitcast_fusion.2), kind=kLoop, calls=%fused_computation.clone.1 | loop fusion | flops 524288 | bytes 3145860 | tf_op jit(solution)/shard_map/while/body/add | solution.py:125
  115.3 1.5 %bitcast_add_fusion.4 = f32[32,64,128]{2,1,0:T(8,128)S(1)} fusion(f32[4,32,64,128]{3,2,1,0:T(8,128)} %get-tuple-element.168, s32[]{:T(128)S(6)} %select_n.51, f32[32,64,128]{2,1,0:T(8,128)S(1)} %get-tuple-element.157, f32[32]{0:T(128)S(1)} %dynamic-slice_bitcast_fusion.2), kind=kLoop, calls=%fused_computation.clone.1 | loop fusion | flops 524288 | bytes 3145860 | tf_op jit(solution)/shard_map/while/body/add | solution.py:125
  116.7 0.2 multiply_convert_fusion.3
  116.9 1.8 %convolution_bitcast_fusion = f32[2,1024,1,256]{1,3,0,2:T(8,128)} fusion(bf16[2,1024,128]{2,1,0:T(8,128)(2,1)S(1)} %bitcast.82, bf16[2,256,256]{2,1,0:T(8,128)(2,1)S(1)} %multiply_convert_fusion.4), kind=kOutput, calls=%fused_computation.38 | convolution fusion | flops 134217728 | bytes 2752512 | tf_op jit(solution)/shard_map/gbcn,gnbt->gcbt/dot_general | solution.py:87
  118.7 1.9 %copy.38 = f32[2,1024,1,256]{3,1,0,2:T(8,128)S(1)} copy(f32[2,1024,1,256]{1,3,0,2:T(8,128)} %convolution_bitcast_fusion) | data formatting | bytes 4194304 | tf_op jit(solution)/shard_map/gbcn,gnbt->gcbt/transpose | solution.py:87
  120.6 0.0 copy-start.2
  120.7 2.2 %fusion.21 = bf16[2048,256]{1,0:T(8,128)(2,1)S(1)} fusion(f32[2,16,256,64]{2,3,1,0:T(8,128)} %fusion, f32[2,1024,1,256]{3,1,0,2:T(8,128)S(1)} %copy.38, f32[32,256]{1,0:T(8,128)S(1)} %get-tuple-element.101, f32[2048]{0:T(1024)S(1)} %mul.257, bf16[2048,256]{1,0:T(8,128)(2,1)S(1)} %multiply_convert_fusion.2), kind=kLoop, calls=%fused_computation.32 | loop fusion | flops 3145728 | bytes 6332416 | tf_op jit(solution)/shard_map/convert_element_type | solution.py:174
  122.8 0.0 copy-done.2
  122.9 1.7 %fusion.23 = bf16[2048,256]{1,0:T(8,128)(2,1)} fusion(bf16[2048,256]{1,0:T(8,128)(2,1)S(1)} %copy-done.2, bf16[2048,256]{1,0:T(8,128)(2,1)S(1)} %fusion.21), kind=kLoop, calls=%fused_computation.37 | loop fusion | flops 4194304 | bytes 3145728 | tf_op jit(solution)/shard_map/convert_element_type | solution.py:176
  (21 shorter events, 0.3 us)
Async XLA Ops:
  6.5 9.2 %copy-start = (f32[8,256]{1,0:T(8,128)S(1)}, f32[8,256]{1,0:T(8,128)}, u32[]{:S(2)}) copy-start(f32[8,256]{1,0:T(8,128)} %param.20) | copy-start | bytes 24580
  6.5 9.2 %copy-start.1 = (bf16[2048,256]{1,0:T(8,128)(2,1)S(1)}, bf16[2048,256]{1,0:T(8,128)(2,1)}, u32[]{:S(2)}) copy-start(bf16[2048,256]{1,0:T(8,128)(2,1)} %param.13) | copy-start | bytes 3145732
  6.5 6.0 %copy-start.8 = (f32[32]{0:T(128)S(1)}, f32[32]{0:T(128)}, u32[]{:S(2)}) copy-start(f32[32]{0:T(128)} %param.22) | copy-start | bytes 388
  6.5 6.0 %copy-start.3 = (bf16[32,256]{1,0:T(8,128)(2,1)S(1)}, bf16[32,256]{1,0:T(8,128)(2,1)}, u32[]{:S(2)}) copy-start(bf16[32,256]{1,0:T(8,128)(2,1)} %param.16) | copy-start | bytes 49156
  6.5 6.1 %copy-start.6 = (f32[32]{0:T(128)S(1)}, f32[32]{0:T(128)}, u32[]{:S(2)}) copy-start(f32[32]{0:T(128)} %param.21) | copy-start | bytes 388
  6.5 7.2 %copy-start.4 = (f32[2048,4]{0,1:T(4,128)S(1)}, f32[2048,4]{0,1:T(4,128)}, u32[]{:S(2)}) copy-start(f32[2048,4]{0,1:T(4,128)} %param.17) | copy-start | bytes 98308
  6.6 105.5 %all-gather.3.cloned.1.call-start = ((), (), s32[]{:S(2)}) async-start(), calls=%async_computation | async-start | bytes 5242880 | tf_op jit(solution)/shard_map/all_gather | solution.py:21
  7.7 8.2 %collective-permute-start = (bf16[2,256,3]{2,1,0:T(8,128)(2,1)S(1)}, bf16[2,256,3]{2,1,0:T(8,128)(2,1)S(1)}, u32[]{:S(2)}, u32[]{:S(2)}) collective-permute-start(bf16[2,256,3]{2,1,0:T(8,128)(2,1)S(1)} %constant_dynamic-slice_fusion.2), channel_id=1, source_target_pairs={{0,4},{4,8},{8,12},{1,5},{5,9},{9,13},{2,6},{6,10},{10,14},{3,7},{... | collective-permute-start | bytes 9224 | tf_op jit(solution)/shard_map/ppermute | solution.py:16
  10.3 16.2 %collective-permute-start.1 = (bf16[2048,3]{1,0:T(8,128)(2,1)S(1)}, bf16[2048,3]{1,0:T(8,128)(2,1)S(1)}, u32[]{:S(2)}, u32[]{:S(2)}) collective-permute-start(bf16[2048,3]{1,0:T(8,128)(2,1)S(1)} %slice.76), channel_id=1, source_target_pairs={{0,4},{4,8},{8,12},{1,5},{5,9},{9,13},{2,6},{6,10},{10,14},{3,7},{... | collective-permute-start | bytes 36872 | tf_op jit(solution)/shard_map/ppermute | solution.py:16
  15.9 10.6 %copy-start.5 = (f32[2048]{0:T(1024)S(1)}, f32[2048]{0:T(1024)}, u32[]{:S(2)}) copy-start(f32[2048]{0:T(1024)} %param.18) | copy-start | bytes 24580
  31.5 1.2 copy-start.9
  31.5 11.2 %copy-start.7 = (f32[32]{0:T(128)S(1)}, f32[32]{0:T(128)}, u32[]{:S(2)}) copy-start(f32[32]{0:T(128)} %param.23) | copy-start | bytes 388
  120.6 2.2 %copy-start.2 = (bf16[2048,256]{1,0:T(8,128)(2,1)S(1)}, bf16[2048,256]{1,0:T(8,128)(2,1)}, u32[]{:S(2)}) copy-start(bf16[2048,256]{1,0:T(8,128)(2,1)} %param.14) | copy-start | bytes 3145732
Sparse Core Ops, SparseCore 0:
  32.8 79.2 all-gather.2
where the time goes:
time: 132 us; the launch traced here: 131 us
  waiting for transfers between devices  74.1 us (56%)
  other arithmetic  17.8 us (13%)
  between operations  14.5 us (11%)
  blocking collectives  8.27 us (6%)
  local copies, waits for them, and re-layouts  7.12 us (5%)
  matrix products  6.85 us (5%)
  starting transfers between devices  2.62 us (2%)
    all_gather x1, waiting for transfers between devices, prefix(): gathered = jax.tree.map(lambda a: lax.all_gather(a, axis), part)  64.6 us
    ppermute x2, waiting for transfers between devices, passed_along(): return lax.ppermute(block, axis, route)  9.49 us
    unnamed x1, blocking collectives  8.27 us
    add x3, other arithmetic, join_states(): later[0][:, None, None] * earlier[1] + later[1]  4.36 us
    dot_general x1, matrix products, one_step(): jnp.einsum('gucbs,gubts->gucbt', x_part, mixing, preferred_element_type=j...  4.33 us
    convert_element_type x1, other arithmetic, local(): x_conv = causal_filter(x_in.astype(jnp.float32), conv_x_w, conv_x_b, rim_...  4.02 us
  transfers between devices with their start and end apart: 3, of which 2 were waited for; matrix products, arithmetic and copies ran while one was open for 9% of the time, Pallas kernels for 0%

commit v1 on v0

v1 whole, which is shorter than its diff:
```python
import functools
import math

import jax
import jax.numpy as jnp
from jax import lax
from jax.experimental import pallas as pl
from jax.experimental.pallas import tpu as pltpu
from jax.sharding import PartitionSpec as P

HEADS = 128
GROUPS = 8
BLOCK = 256
LANES = 128
LOG2E = 1.4426950408889634
F32 = jnp.float32
BF16 = jnp.bfloat16


def dot(a, b, ca, cb, precision=None):
    return lax.dot_general(
        a, b, (((ca,), (cb,)), ((), ())), preferred_element_type=F32, precision=precision
    )


def silu(v):
    half = 0.5 * v
    return half + half * jnp.tanh(half)


def one_hot_rows(rows, first, kernel_size):
    r = lax.broadcasted_iota(jnp.int32, (rows, LANES), 0) - first
    lane = lax.broadcasted_iota(jnp.int32, (rows, LANES), 1)
    keep = kernel_size - 1
    hit = (r >= 0) & (r < keep) & (lane == r + LANES - keep)
    return jnp.where(hit, 1.0, 0.0).astype(BF16)


def conv_rows(values, before, columns, kernel_size):
    lane = lax.broadcasted_iota(jnp.int32, (values.shape[0], LANES), 1)
    first, second = values[:, :LANES], values[:, LANES:]
    bias = columns[:, kernel_size : kernel_size + 1]
    last = columns[:, kernel_size - 1 : kernel_size]
    out0 = bias + last * first
    out1 = bias + last * second
    for d in range(1, kernel_size):
        tap = columns[:, kernel_size - 1 - d : kernel_size - d]
        tail = lane >= LANES - d
        out0 = out0 + tap * pltpu.roll(jnp.where(tail, before, first), d, 1)
        out1 = out1 + tap * pltpu.roll(jnp.where(tail, first, second), d, 1)
    return silu(jnp.concatenate([out0, out1], axis=1)).astype(BF16)


def mixer(
    cfg,
    x_ref, bc_hbm, dt_ref, wx_ref, bx_ref, wbc_ref, bbc_ref, dtb_ref, alog_ref, dskip_ref,
    y_ref,
    bc_buf, halo_out, halo_in, wcol, xc, bcc, gram, fresh, send_buf, recv_buf,
    cum2, ecum, gain, decay, cols, acc,
    bc_sem, halo_sem, send_sem, recv_sem,
):
    n_cp, heads, hc, kernel_size, lgroups, state = cfg
    channels = x_ref.shape[0]
    head_dim = channels // heads
    rows = hc * head_dim
    chunks = heads // hc
    per_group = heads // lgroups
    me = lax.axis_index("cp")
    nxt = lax.rem(me + 1, n_cp)
    prv = lax.rem(me + n_cp - 1, n_cp)
    first_group = lax.axis_index("tensor") * heads // (HEADS // GROUPS)
    has_prev = me > 0
    has_next = me < n_cp - 1
    xblocks = channels // LANES
    bblocks = 2 * state // LANES
    hrows = halo_out.shape[0]

    bc_copy = pltpu.make_async_copy(bc_hbm.at[pl.ds(first_group, lgroups)], bc_buf, bc_sem)
    bc_copy.start()

    barrier = pltpu.get_barrier_semaphore()

    @pl.when(has_prev)
    def _():
        pl.semaphore_signal(barrier, inc=1, device_id={"cp": prv})

    @pl.when(has_next)
    def _():
        pl.semaphore_signal(barrier, inc=1, device_id={"cp": nxt})

    halo = jnp.zeros((hrows, LANES), F32)
    for b in range(xblocks):
        tail = x_ref[b * LANES : (b + 1) * LANES, BLOCK - LANES :]
        halo = halo + dot(one_hot_rows(hrows, 4 * b, kernel_size), tail, 1, 1)
    bc_copy.wait()
    for g in range(lgroups):
        for k in range(bblocks):
            tail = bc_buf[g, k * LANES : (k + 1) * LANES, BLOCK - LANES :]
            at = 4 * (xblocks + g * bblocks + k)
            halo = halo + dot(one_hot_rows(hrows, at, kernel_size), tail, 1, 1)
    halo_out[...] = halo.astype(BF16)

    pl.semaphore_wait(barrier, has_prev.astype(jnp.int32) + has_next.astype(jnp.int32))

    halo_copy = pltpu.make_async_remote_copy(
        src_ref=halo_out, dst_ref=halo_in, send_sem=halo_sem.at[0], recv_sem=halo_sem.at[1],
        device_id={"cp": nxt},
    )

    def state_copy(j):
        return pltpu.make_async_remote_copy(
            src_ref=send_buf.at[j], dst_ref=recv_buf.at[j],
            send_sem=send_sem.at[j], recv_sem=recv_sem.at[j], device_id={"cp": nxt},
        )

    @pl.when(has_next)
    def _():
        halo_copy.start()

    @pl.when(jnp.logical_not(has_prev))
    def _():
        halo_in[...] = jnp.zeros_like(halo_in)
        recv_buf[...] = jnp.zeros_like(recv_buf)

    row = lax.broadcasted_iota(jnp.int32, (heads, BLOCK), 0)
    bias = jnp.zeros((heads, BLOCK), F32)
    alog = jnp.zeros((heads, BLOCK), F32)
    for h in range(heads):
        bias = jnp.where(row == h, dtb_ref[h], bias)
        alog = jnp.where(row == h, alog_ref[h], alog)
    grown = jnp.exp(dt_ref[...].astype(F32) + bias)
    series = grown * (1.0 - grown * (0.5 - grown * (1.0 / 3.0 - 0.25 * grown)))
    delta = jnp.where(grown < 0.01, series, jnp.log(1.0 + grown))
    s_at = lax.broadcasted_iota(jnp.int32, (BLOCK, BLOCK), 0)
    t_at = lax.broadcasted_iota(jnp.int32, (BLOCK, BLOCK), 1)
    upper = jnp.where(s_at <= t_at, 1.0, 0.0)
    cum = dot(
        delta * (jnp.exp(alog) * (-LOG2E)), upper, 1, 0, precision=lax.Precision.HIGHEST
    )
    end = cum[:, BLOCK - 1 : BLOCK]
    cum2[...] = cum
    ecum[...] = jnp.exp2(cum)
    gain[...] = delta * jnp.exp2(end - cum)
    decay[...] = jnp.broadcast_to(jnp.exp2(end), (heads, LANES))
    source = jnp.transpose(jnp.log2(delta) - cum)
    for j in range(chunks):
        cols[j] = source[:, j * hc : (j + 1) * hc]

    def columns_of(taps, offsets):
        width = taps.shape[1]
        fill = jnp.zeros((8 - kernel_size - 1, width), F32)
        return jnp.transpose(jnp.concatenate([taps, offsets, fill], axis=0))

    wcol[...] = columns_of(wx_ref[...], bx_ref[...])

    @pl.when(has_prev)
    def _():
        halo_copy.wait_recv()

    def before_of(block):
        return dot(halo_in[...], one_hot_rows(hrows, 4 * block, kernel_size), 0, 0)

    for g in range(lgroups):
        columns = columns_of(wbc_ref[first_group + g], bbc_ref[pl.ds(first_group + g, 1), :])
        for k in range(bblocks):
            at = slice(k * LANES, (k + 1) * LANES)
            bcc[g, at, :] = conv_rows(
                bc_buf[g, at, :].astype(F32), before_of(xblocks + g * bblocks + k),
                columns[at], kernel_size,
            )
        gram[g] = dot(bcc[g, :state, :], bcc[g, state:, :], 0, 0)

    def spread(ref, j):
        return jnp.concatenate(
            [
                jnp.broadcast_to(ref[pl.ds(j * hc + i, 1), :], (head_dim, ref.shape[1]))
                for i in range(hc)
            ],
            axis=0,
        )

    def prepare(j, carry):
        start = pl.multiple_of(j * rows, rows)
        for b in range(rows // LANES):
            at = pl.ds(pl.multiple_of(start + b * LANES, LANES), LANES)
            xc[at, :] = conv_rows(
                x_ref[at, :].astype(F32), before_of(j * (rows // LANES) + b), wcol[at, :], kernel_size
            )
        wide = xc[pl.ds(start, rows), :].astype(F32)
        weighted = (wide * spread(gain, j)).astype(BF16)
        new = dot(weighted, bcc[j * hc // per_group, :state, :], 1, 1)
        fresh[j] = new

        @pl.when(jnp.logical_not(has_prev) & has_next)
        def _():
            send_buf[j] = new.astype(BF16)
            state_copy(j).start()

        return carry

    lax.fori_loop(0, chunks, prepare, 0)

    half_s = lax.broadcasted_iota(jnp.int32, (LANES, LANES), 0)
    half_t = lax.broadcasted_iota(jnp.int32, (LANES, LANES), 1)
    causal = half_s <= half_t
    empty = jnp.zeros((LANES, LANES), BF16)

    def finish(j, carry):
        start = pl.multiple_of(j * rows, rows)
        g = j * hc // per_group
        for i in range(hc):
            h = j * hc + i
            at = pl.ds(pl.multiple_of(start + i * head_dim, head_dim), head_dim)
            to = cum2[pl.ds(h, 1), :]
            of = cols[j, :, i : i + 1]
            near0 = jnp.where(causal, jnp.exp2(to[:, :LANES] + of[:LANES]), 0.0)
            far = jnp.exp2(to[:, LANES:] + of[:LANES])
            near1 = jnp.where(causal, jnp.exp2(to[:, LANES:] + of[LANES:]), 0.0)
            m00 = (near0 * gram[g, :LANES, :LANES]).astype(BF16)
            m01 = (far * gram[g, :LANES, LANES:]).astype(BF16)
            m11 = (near1 * gram[g, LANES:, LANES:]).astype(BF16)
            mixing = jnp.concatenate(
                [jnp.concatenate([m00, m01], axis=1), jnp.concatenate([empty, m11], axis=1)], axis=0
            )
            own = xc[at, :]
            acc[i * head_dim : (i + 1) * head_dim, :] = (
                dot(own, mixing, 1, 0) + dskip_ref[h] * own.astype(F32)
            )

        @pl.when(has_prev)
        def _():
            state_copy(j).wait_recv()

        @pl.when(has_prev & has_next)
        def _():
            passed = spread(decay, j) * recv_buf[j].astype(F32) + fresh[j]
            send_buf[j] = passed.astype(BF16)
            state_copy(j).start()

        carried = dot(recv_buf[j], bcc[g, state:, :], 1, 0)
        y_ref[pl.ds(start, rows), :] = (acc[...] + spread(ecum, j) * carried).astype(BF16)
        return carry

    lax.fori_loop(0, chunks, finish, 0)

    @pl.when(has_next)
    def _():
        halo_copy.wait_send()

        def drain(j, carry):
            state_copy(j).wait_send()
            return carry

        lax.fori_loop(0, chunks, drain, 0)


def local(
    x_in, z_gate, bc_in, dt_raw, conv_x_w, conv_x_b, conv_bc_w, conv_bc_b, dt_bias, a_log, d_skip
):
    heads = dt_raw.shape[0]
    length = dt_raw.shape[1]
    assert length == BLOCK
    channels = x_in.shape[0]
    state = bc_in.shape[1] // 2
    kernel_size = conv_x_w.shape[1]
    lgroups = max(1, heads * GROUPS // HEADS)
    hc = math.gcd(heads // lgroups, 4)
    chunks = heads // hc
    rows = channels // chunks
    n_cp = lax.axis_size("cp")
    blocks = channels // LANES + lgroups * 2 * state // LANES
    hrows = -(-4 * blocks // 16) * 16
    vmem = pl.BlockSpec(memory_space=pltpu.VMEM)
    smem = pl.BlockSpec(memory_space=pltpu.SMEM)
    y = pl.pallas_call(
        functools.partial(mixer, (n_cp, heads, hc, kernel_size, lgroups, state)),
        out_shape=jax.ShapeDtypeStruct((channels, length), BF16),
        in_specs=[vmem, pl.BlockSpec(memory_space=pl.ANY)] + [vmem] * 5 + [smem] * 3,
        out_specs=vmem,
        scratch_shapes=[
            pltpu.VMEM((lgroups, 2 * state, length), BF16),
            pltpu.VMEM((hrows, LANES), BF16),
            pltpu.VMEM((hrows, LANES), BF16),
            pltpu.VMEM((channels, 8), F32),
            pltpu.VMEM((channels, length), BF16),
            pltpu.VMEM((lgroups, 2 * state, length), BF16),
            pltpu.VMEM((lgroups, length, length), F32),
            pltpu.VMEM((chunks, rows, state), F32),
            pltpu.VMEM((chunks, rows, state), BF16),
            pltpu.VMEM((chunks, rows, state), BF16),
            pltpu.VMEM((heads, length), F32),
            pltpu.VMEM((heads, length), F32),
            pltpu.VMEM((heads, length), F32),
            pltpu.VMEM((heads, LANES), F32),
            pltpu.VMEM((chunks, length, hc), F32),
            pltpu.VMEM((rows, length), F32),
            pltpu.SemaphoreType.DMA,
            pltpu.SemaphoreType.DMA((2,)),
            pltpu.SemaphoreType.DMA((chunks,)),
            pltpu.SemaphoreType.DMA((chunks,)),
        ],
        compiler_params=pltpu.CompilerParams(
            collective_id=0, has_side_effects=True, vmem_limit_bytes=48 * 2**20
        ),
        name="mixer",
    )(
        x_in, bc_in, dt_raw, conv_x_w.T, conv_x_b[None], jnp.swapaxes(conv_bc_w, 1, 2), conv_bc_b,
        dt_bias, a_log, d_skip,
    )
    gate = z_gate.astype(F32)
    return (y.astype(F32) * jax.nn.silu(gate)).astype(BF16)


def solution(mesh):
    return jax.shard_map(
        local,
        mesh=mesh,
        in_specs=(
            P("tensor", ("dp", "cp")),
            P("tensor", ("dp", "cp")),
            P(None, None, ("dp", "cp")),
            P("tensor", ("dp", "cp")),
            P("tensor", None),
            P("tensor"),
            P(),
            P(),
            P("tensor"),
            P("tensor"),
            P("tensor"),
        ),
        out_specs=P("tensor", ("dp", "cp")),
        check_vma=False,
    )
```

time: 132 us -> 36.8 us (0.28)
  waiting for transfers between devices: 74.1 us -> 0 us
  Pallas kernels: 0 us -> 26.6 us
  other arithmetic: 17.8 us -> 1.65 us
  between operations: 14.5 us -> 0.03 us
  blocking collectives: 8.27 us -> 0 us
  matrix products: 6.85 us -> 0 us
  starting transfers between devices: 2.62 us -> 0 us
    all_gather x1 -> x0, waiting for transfers between devices: 64.6 us -> none  [prefix(): gathered = jax.tree.map(lambda a: lax.all_gather(a, axis), part)]
    pallas_call x0 -> x1, Pallas kernels: none -> 26.6 us  [local(): pl.pallas_call(functools.partial(mixer, (n_cp, heads, hc, kernel_size, lg...]
    ppermute x2 -> x0, waiting for transfers between devices: 9.49 us -> none  [passed_along(): return lax.ppermute(block, axis, route)]
    convert_element_type x10 -> x1, other arithmetic: 10.6 us -> 1.65 us  [local(): return (y.astype(F32) * jax.nn.silu(gate)).astype(BF16)]
    unnamed x1 -> x0, blocking collectives: 8.27 us -> none
    unnamed x25 -> x22, local copies, waits for them, and re-layouts: 0.96 us -> 8.04 us
    dot_general x4 -> x0, matrix products: 6.85 us -> none  [the longest x1 4.33 us: one_step(): jnp.einsum('gucbs,gubts->gucbt', x_part, mixing, preferred_element_type=j...]
    add x4 -> x0, other arithmetic: 5.46 us -> none  [the longest x3 4.36 us: join_states(): later[0][:, None, None] * earlier[1] + later[1]]
  transfers between devices with their start and end apart: 3 -> 0, of which waited for: 2 -> 0; matrix products, arithmetic and copies ran while one was open for 9% -> 0% of each run, Pallas kernels for 0% -> 0%
where the time goes in v1:
time: 36.8 us; the launch traced here: 36.3 us
  Pallas kernels  26.6 us (72%)
  local copies, waits for them, and re-layouts  8.04 us (22%)
  other arithmetic  1.65 us (4%)
    pallas_call x1, Pallas kernels, local(): pl.pallas_call(functools.partial(mixer, (n_cp, heads, hc, kernel_size, lg...  26.6 us
    unnamed x22, local copies, waits for them, and re-layouts  8.04 us
    convert_element_type x1, other arithmetic, local(): return (y.astype(F32) * jax.nn.silu(gate)).astype(BF16)  1.65 us

profile of v1, /device:TPU:24, one launch (start us, length us, event | category | flops | bytes accessed | tf_op | source)
XLA Modules:
  0.0 36.3 jit_solution(8677852619458793914)
XLA Ops:
  0.0 0.0 copy-start
  0.0 1.2 %copy-done = bf16[2048,256]{1,0:T(8,128)(2,1)S(1)} copy-done((bf16[2048,256]{1,0:T(8,128)(2,1)S(1)}, bf16[2048,256]{1,0:T(8,128)(2,1)}, u32[]{:S(2)}) %copy-start) | copy-done | bytes 1048600
  1.2 0.0 copy-start.1
  1.2 1.2 %copy-done.1 = bf16[8,256,256]{2,1,0:T(8,128)(2,1)S(1)} copy-done((bf16[8,256,256]{2,1,0:T(8,128)(2,1)S(1)}, bf16[8,256,256]{2,1,0:T(8,128)(2,1)}, u32[]{:S(2)}) %copy-start.1) | copy-done | bytes 1048600
  2.5 0.0 copy-start.2
  2.5 0.8 %copy-done.2 = f32[2048,4]{0,1:T(4,128)S(1)} copy-done((f32[2048,4]{0,1:T(4,128)S(1)}, f32[2048,4]{0,1:T(4,128)}, u32[]{:S(2)}) %copy-start.2) | copy-done | bytes 32792
  3.2 0.0 copy-start.3
  3.2 0.8 %copy-done.3 = f32[8,256,4]{1,2,0:T(4,128)S(1)} copy-done((f32[8,256,4]{1,2,0:T(4,128)S(1)}, f32[8,256,4]{1,2,0:T(4,128)}, u32[]{:S(2)}) %copy-start.3) | copy-done | bytes 32792
  4.0 0.0 copy-start.4
  4.0 0.7 %copy-done.4 = bf16[32,256]{1,0:T(8,128)(2,1)S(1)} copy-done((bf16[32,256]{1,0:T(8,128)(2,1)S(1)}, bf16[32,256]{1,0:T(8,128)(2,1)}, u32[]{:S(2)}) %copy-start.4) | copy-done | bytes 16408
  4.7 0.0 copy-start.5
  4.7 0.7 %copy-done.5 = f32[2048]{0:T(1024)S(1)} copy-done((f32[2048]{0:T(1024)S(1)}, f32[2048]{0:T(1024)}, u32[]{:S(2)}) %copy-start.5) | copy-done | bytes 8216
  5.4 0.0 copy-start.6
  5.4 0.7 %copy-done.6 = f32[8,256]{1,0:T(8,128)S(1)} copy-done((f32[8,256]{1,0:T(8,128)S(1)}, f32[8,256]{1,0:T(8,128)}, u32[]{:S(2)}) %copy-start.6) | copy-done | bytes 8216
  6.1 0.0 copy-start.7
  6.1 0.7 %copy-done.7 = f32[32]{0:T(128)S(1)} copy-done((f32[32]{0:T(128)S(1)}, f32[32]{0:T(128)}, u32[]{:S(2)}) %copy-start.7) | copy-done | bytes 152
  6.7 0.0 copy-start.8
  6.7 0.7 %copy-done.8 = f32[32]{0:T(128)S(1)} copy-done((f32[32]{0:T(128)S(1)}, f32[32]{0:T(128)}, u32[]{:S(2)}) %copy-start.8) | copy-done | bytes 152
  7.4 0.0 copy-start.9
  7.4 0.7 %copy-done.9 = f32[32]{0:T(128)S(1)} copy-done((f32[32]{0:T(128)S(1)}, f32[32]{0:T(128)}, u32[]{:S(2)}) %copy-start.9) | copy-done | bytes 152
  8.0 0.0 copy-start.10
  8.1 26.6 %mixer.1 = bf16[2048,256]{1,0:T(8,128)(2,1)S(1)} custom-call(bf16[2048,256]{1,0:T(8,128)(2,1)S(1)} %copy-done, bf16[8,256,256]{2,1,0:T(8,128)(2,1)S(1)} %copy-done.1, bf16[32,256]{1,0:T(8,128)(2,1)S(1)} %copy-done.4, f32[4,2048]{1,0:T(4,128)S(1)} %bitcast.3, f32[1,2048]{1,0:T(1,128)S(1)} %bitcast.5, f32[8,4,256]{2,1,0:T(4,128)S(1)} %bitcast.4, ...), custom_call_target="tpu_custom_call" | custom-call | tf_op jit(solution)/shard_map/mixer/pallas_call | solution.py:275
  34.6 0.0 copy-done.10
  34.6 1.6 %fusion.4 = bf16[2048,256]{1,0:T(8,128)(2,1)} fusion(bf16[2048,256]{1,0:T(8,128)(2,1)S(1)} %copy-done.10, bf16[2048,256]{1,0:T(8,128)(2,1)S(1)} %mixer.1), kind=kLoop, calls=%fused_computation.6 | loop fusion | flops 4194304 | bytes 3145728 | tf_op jit(solution)/shard_map/convert_element_type | solution.py:311
Async XLA Ops:
  0.0 1.2 %copy-start = (bf16[2048,256]{1,0:T(8,128)(2,1)S(1)}, bf16[2048,256]{1,0:T(8,128)(2,1)}, u32[]{:S(2)}) copy-start(bf16[2048,256]{1,0:T(8,128)(2,1)} %x_ref.1) | copy-start | bytes 3145732
  1.2 1.2 %copy-start.1 = (bf16[8,256,256]{2,1,0:T(8,128)(2,1)S(1)}, bf16[8,256,256]{2,1,0:T(8,128)(2,1)}, u32[]{:S(2)}) copy-start(bf16[8,256,256]{2,1,0:T(8,128)(2,1)} %bc_hbm.1) | copy-start | bytes 3145732
  2.5 0.8 %copy-start.2 = (f32[2048,4]{0,1:T(4,128)S(1)}, f32[2048,4]{0,1:T(4,128)}, u32[]{:S(2)}) copy-start(f32[2048,4]{0,1:T(4,128)} %param.15) | copy-start | bytes 98308
  3.2 0.8 %copy-start.3 = (f32[8,256,4]{1,2,0:T(4,128)S(1)}, f32[8,256,4]{1,2,0:T(4,128)}, u32[]{:S(2)}) copy-start(f32[8,256,4]{1,2,0:T(4,128)} %param.17) | copy-start | bytes 98308
  4.0 0.7 %copy-start.4 = (bf16[32,256]{1,0:T(8,128)(2,1)S(1)}, bf16[32,256]{1,0:T(8,128)(2,1)}, u32[]{:S(2)}) copy-start(bf16[32,256]{1,0:T(8,128)(2,1)} %dt_ref.1) | copy-start | bytes 49156
  4.7 0.7 %copy-start.5 = (f32[2048]{0:T(1024)S(1)}, f32[2048]{0:T(1024)}, u32[]{:S(2)}) copy-start(f32[2048]{0:T(1024)} %param.16) | copy-start | bytes 24580
  5.4 0.7 %copy-start.6 = (f32[8,256]{1,0:T(8,128)S(1)}, f32[8,256]{1,0:T(8,128)}, u32[]{:S(2)}) copy-start(f32[8,256]{1,0:T(8,128)} %bbc_ref.1) | copy-start | bytes 24580
  6.1 0.7 %copy-start.7 = (f32[32]{0:T(128)S(1)}, f32[32]{0:T(128)}, u32[]{:S(2)}) copy-start(f32[32]{0:T(128)} %dtb_ref.1) | copy-start | bytes 388
  6.7 0.7 %copy-start.8 = (f32[32]{0:T(128)S(1)}, f32[32]{0:T(128)}, u32[]{:S(2)}) copy-start(f32[32]{0:T(128)} %alog_ref.1) | copy-start | bytes 388
  7.4 0.7 %copy-start.9 = (f32[32]{0:T(128)S(1)}, f32[32]{0:T(128)}, u32[]{:S(2)}) copy-start(f32[32]{0:T(128)} %dskip_ref.1) | copy-start | bytes 388
  8.0 26.6 %copy-start.10 = (bf16[2048,256]{1,0:T(8,128)(2,1)S(1)}, bf16[2048,256]{1,0:T(8,128)(2,1)}, u32[]{:S(2)}) copy-start(bf16[2048,256]{1,0:T(8,128)(2,1)} %param.12) | copy-start | bytes 3145732

commit v2 on v1

--- a/solution.py
+++ b/solution.py
@@ -53,11 +53,12 @@
 
 def mixer(
     cfg,
-    x_ref, bc_hbm, dt_ref, wx_ref, bx_ref, wbc_ref, bbc_ref, dtb_ref, alog_ref, dskip_ref,
+    x_hbm, bc_hbm, dt_hbm, wx_hbm, bx_hbm, wbc_hbm, bbc_hbm, dtb_hbm, alog_hbm, dskip_hbm,
     y_ref,
+    x_ref, dt_ref, wx_ref, bx_ref, wbc_ref, bbc_ref, dtb_ref, alog_ref, dskip_ref,
     bc_buf, halo_out, halo_in, wcol, xc, bcc, gram, fresh, send_buf, recv_buf,
-    cum2, ecum, gain, decay, cols, acc,
-    bc_sem, halo_sem, send_sem, recv_sem,
+    cum2, ecum, gain, decay, skip, cols, acc,
+    in_sem, bc_sem, halo_sem, send_sem, recv_sem,
 ):
     n_cp, heads, hc, kernel_size, lgroups, state = cfg
     channels = x_ref.shape[0]
@@ -78,6 +79,20 @@
     bc_copy = pltpu.make_async_copy(bc_hbm.at[pl.ds(first_group, lgroups)], bc_buf, bc_sem)
     bc_copy.start()
 
+    right, left = pl.ds(BLOCK - LANES, LANES), pl.ds(0, LANES)
+    pairs = (
+        (x_hbm.at[:, right], x_ref.at[:, right]),
+        (dt_hbm, dt_ref), (dtb_hbm, dtb_ref), (alog_hbm, alog_ref), (dskip_hbm, dskip_ref),
+        (wx_hbm, wx_ref), (bx_hbm, bx_ref),
+        (wbc_hbm.at[pl.ds(first_group, lgroups)], wbc_ref), (bbc_hbm, bbc_ref),
+        (x_hbm.at[:, left], x_ref.at[:, left]),
+    )
+    loads = [
+        pltpu.make_async_copy(src, dst, in_sem.at[i]) for i, (src, dst) in enumerate(pairs)
+    ]
+    for load in loads:
+        load.start()
+
     barrier = pltpu.get_barrier_semaphore()
 
     @pl.when(has_prev)
@@ -89,6 +104,7 @@
         pl.semaphore_signal(barrier, inc=1, device_id={"cp": nxt})
 
     halo = jnp.zeros((hrows, LANES), F32)
+    loads[0].wait()
     for b in range(xblocks):
         tail = x_ref[b * LANES : (b + 1) * LANES, BLOCK - LANES :]
         halo = halo + dot(one_hot_rows(hrows, 4 * b, kernel_size), tail, 1, 1)
@@ -122,12 +138,16 @@
         halo_in[...] = jnp.zeros_like(halo_in)
         recv_buf[...] = jnp.zeros_like(recv_buf)
 
-    row = lax.broadcasted_iota(jnp.int32, (heads, BLOCK), 0)
-    bias = jnp.zeros((heads, BLOCK), F32)
-    alog = jnp.zeros((heads, BLOCK), F32)
-    for h in range(heads):
-        bias = jnp.where(row == h, dtb_ref[h], bias)
-        alog = jnp.where(row == h, alog_ref[h], alog)
+    for load in loads[1:]:
+        load.wait()
+    vectors = jnp.transpose(
+        jnp.concatenate(
+            [dtb_ref[...], alog_ref[...], dskip_ref[...], jnp.zeros((5, heads), F32)], axis=0
+        )
+    )
+    bias = vectors[:, 0:1]
+    alog = vectors[:, 1:2]
+    skip[...] = jnp.broadcast_to(vectors[:, 2:3], (heads, BLOCK))
     grown = jnp.exp(dt_ref[...].astype(F32) + bias)
     series = grown * (1.0 - grown * (0.5 - grown * (1.0 / 3.0 - 0.25 * grown)))
     delta = jnp.where(grown < 0.01, series, jnp.log(1.0 + grown))
@@ -161,7 +181,7 @@
         return dot(halo_in[...], one_hot_rows(hrows, 4 * block, kernel_size), 0, 0)
 
     for g in range(lgroups):
-        columns = columns_of(wbc_ref[first_group + g], bbc_ref[pl.ds(first_group + g, 1), :])
+        columns = columns_of(wbc_ref[g], bbc_ref[pl.ds(first_group + g, 1), :])
         for k in range(bblocks):
             at = slice(k * LANES, (k + 1) * LANES)
             bcc[g, at, :] = conv_rows(
@@ -224,7 +244,7 @@
             )
             own = xc[at, :]
             acc[i * head_dim : (i + 1) * head_dim, :] = (
-                dot(own, mixing, 1, 0) + dskip_ref[h] * own.astype(F32)
+                dot(own, mixing, 1, 0) + skip[pl.ds(h, 1), :] * own.astype(F32)
             )
 
         @pl.when(has_prev)
@@ -264,20 +284,29 @@
     state = bc_in.shape[1] // 2
     kernel_size = conv_x_w.shape[1]
     lgroups = max(1, heads * GROUPS // HEADS)
-    hc = math.gcd(heads // lgroups, 4)
+    hc = math.gcd(heads // lgroups, 2)
     chunks = heads // hc
     rows = channels // chunks
     n_cp = lax.axis_size("cp")
     blocks = channels // LANES + lgroups * 2 * state // LANES
     hrows = -(-4 * blocks // 16) * 16
     vmem = pl.BlockSpec(memory_space=pltpu.VMEM)
-    smem = pl.BlockSpec(memory_space=pltpu.SMEM)
+    hbm = pl.BlockSpec(memory_space=pltpu.HBM)
     y = pl.pallas_call(
         functools.partial(mixer, (n_cp, heads, hc, kernel_size, lgroups, state)),
         out_shape=jax.ShapeDtypeStruct((channels, length), BF16),
-        in_specs=[vmem, pl.BlockSpec(memory_space=pl.ANY)] + [vmem] * 5 + [smem] * 3,
+        in_specs=[hbm] * 10,
         out_specs=vmem,
         scratch_shapes=[
+            pltpu.VMEM(x_in.shape, BF16),
+            pltpu.VMEM(dt_raw.shape, BF16),
+            pltpu.VMEM((kernel_size, channels), F32),
+            pltpu.VMEM((1, channels), F32),
+            pltpu.VMEM((lgroups, kernel_size, 2 * state), F32),
+            pltpu.VMEM(conv_bc_b.shape, F32),
+            pltpu.VMEM((1, heads), F32),
+            pltpu.VMEM((1, heads), F32),
+            pltpu.VMEM((1, heads), F32),
             pltpu.VMEM((lgroups, 2 * state, length), BF16),
             pltpu.VMEM((hrows, LANES), BF16),
             pltpu.VMEM((hrows, LANES), BF16),
@@ -292,20 +321,22 @@
             pltpu.VMEM((heads, length), F32),
             pltpu.VMEM((heads, length), F32),
             pltpu.VMEM((heads, LANES), F32),
+            pltpu.VMEM((heads, length), F32),
             pltpu.VMEM((chunks, length, hc), F32),
             pltpu.VMEM((rows, length), F32),
+            pltpu.SemaphoreType.DMA((10,)),
             pltpu.SemaphoreType.DMA,
             pltpu.SemaphoreType.DMA((2,)),
             pltpu.SemaphoreType.DMA((chunks,)),
             pltpu.SemaphoreType.DMA((chunks,)),
         ],
         compiler_params=pltpu.CompilerParams(
-            collective_id=0, has_side_effects=True, vmem_limit_bytes=48 * 2**20
+            collective_id=0, has_side_effects=True, vmem_limit_bytes=60 * 1024 * 1024
         ),
         name="mixer",
     )(
         x_in, bc_in, dt_raw, conv_x_w.T, conv_x_b[None], jnp.swapaxes(conv_bc_w, 1, 2), conv_bc_b,
-        dt_bias, a_log, d_skip,
+        dt_bias[None], a_log[None], d_skip[None],
     )
     gate = z_gate.astype(F32)
     return (y.astype(F32) * jax.nn.silu(gate)).astype(BF16)

time: 36.8 us -> 32.6 us (0.89)
  local copies, waits for them, and re-layouts: 8.04 us -> 0.01 us
  Pallas kernels: 26.6 us -> 29.4 us
  other arithmetic: 1.65 us -> 2.86 us
    unnamed x22 -> x2, local copies, waits for them, and re-layouts: 8.04 us -> 0.01 us
    pallas_call x1, Pallas kernels: 26.6 us -> 29.4 us  [local(): pl.pallas_call(functools.partial(mixer, (n_cp, heads, hc, kernel_size, lg...]
    convert_element_type x1, other arithmetic: 1.65 us -> 2.86 us  [local(): return (y.astype(F32) * jax.nn.silu(gate)).astype(BF16)]
where the time goes in v2:
time: 32.6 us; the launch traced here: 32.2 us
  Pallas kernels  29.4 us (90%)
  other arithmetic  2.86 us (9%)
    pallas_call x1, Pallas kernels, local(): pl.pallas_call(functools.partial(mixer, (n_cp, heads, hc, kernel_size, lg...  29.4 us
    convert_element_type x1, other arithmetic, local(): return (y.astype(F32) * jax.nn.silu(gate)).astype(BF16)  2.86 us

profile of v2, /device:TPU:24, one launch (start us, length us, event | category | flops | bytes accessed | tf_op | source)
XLA Modules:
  0.0 32.2 jit_solution(13744943023939185312)
XLA Ops:
  0.0 0.0 copy-start
  0.0 29.4 %mixer.1 = bf16[2048,256]{1,0:T(8,128)(2,1)} custom-call(bf16[2048,256]{1,0:T(8,128)(2,1)} %x_hbm.1, bf16[8,256,256]{2,1,0:T(8,128)(2,1)} %bc_hbm.1, bf16[32,256]{1,0:T(8,128)(2,1)} %dt_hbm.1, f32[4,2048]{1,0:T(4,128)} %bitcast.6, f32[1,2048]{1,0:T(1,128)} %bitcast.8, f32[8,4,256]{2,1,0:T(4,128)} %bitcast.7, f32[8,256]{1,0:T(8,128)} %bbc_hbm.1, ...), custom_call_target="tpu_custom_call" | custom-call | tf_op jit(solution)/shard_map/mixer/pallas_call | solution.py:295
  29.4 0.0 copy-done
  29.4 2.9 %fusion.4 = bf16[2048,256]{1,0:T(8,128)(2,1)} fusion(bf16[2048,256]{1,0:T(8,128)(2,1)S(1)} %copy-done, bf16[2048,256]{1,0:T(8,128)(2,1)} %mixer.1), kind=kLoop, calls=%fused_computation.6 | loop fusion | flops 4194304 | bytes 3145728 | tf_op jit(solution)/shard_map/convert_element_type | solution.py:342
Async XLA Ops:
  0.0 29.4 %copy-start = (bf16[2048,256]{1,0:T(8,128)(2,1)S(1)}, bf16[2048,256]{1,0:T(8,128)(2,1)}, u32[]{:S(2)}) copy-start(bf16[2048,256]{1,0:T(8,128)(2,1)} %param.12) | copy-start | bytes 3145732
